TPU v7x, 32 devices: a whole 2x2x4 slice. The times are simulated.
32 devices in a mesh: rep: 2 (over y), dev: 4 (over z), col: 4 (over x, core).
Axes of the slice: x: 2, y: 2, z: 4, core: 2. Of those that a mesh axis runs over, the one named last changes fastest.
Arguments:
- queries: bfloat16 [256, 8192], P(('rep', 'dev'), 'col'), parts along dimension 0
- kv_pages: bfloat16 [768, 8, 2, 128, 128], P(('rep', 'dev'), 'col'), parts along dimension 0
- page_table: int32 [256, 3], P(('rep', 'dev')), parts along dimension 0, may hold values from 0 to 95, as said below
- seq_lengths: int32 [256], P(('rep', 'dev')), parts along dimension 0, may hold values from 2 to 384, as said below
- ffn_seat: int32 [256], P('rep'), parts along dimension 0, may hold values from 0 to 127, each once
- resid: bfloat16 [256, 8192], P(('rep', 'col'), 'dev'), parts along dimension 0, may hold values from -6 to 6
- w_out: bfloat16 [8192, 8192], P('col', 'dev'), may hold values from -0.0625 to 0.0625
- norm_gain: float32 [8192], P('dev'), may hold values from 0.25 to 1.75
- w_gate: bfloat16 [8192, 14336], P('dev', 'col'), may hold values from -0.0625 to 0.0625
- w_up: bfloat16 [8192, 14336], P('dev', 'col'), may hold values from -0.0625 to 0.0625
- w_down: bfloat16 [14336, 8192], P('col', 'dev'), may hold values from -0.046875 to 0.046875
Outputs:
- layer_out: bfloat16 [256, 8192], P(('rep', 'col'), 'dev'), parts along dimension 0
There are 2 independent parts, one for each index of `rep`. A program takes and returns all parts, laid end to end along the dimension named above; an argument that names none is the same for every part. Nothing has to cross between parts.
Inputs may be any that keep to these rules, and one draw needn't show every extreme that they name: `page_table`: the 32 rows of one dev index hold each block 0 to 95 of that index's pool exactly once. `seq_lengths`: the first sequence has 384 cached tokens.
All inputs are finite; a program needn't handle non-finite values.
Results may differ from a plain program's by a relative error of at most 0.017.
Values may be sent and summed in bfloat16 or wider, within the bound.
A program may use at most 128 MiB of HBM per device.

v0:
```python
import jax
import jax.numpy as jnp
from jax import lax
from jax.sharding import PartitionSpec as P


def on_device(
    queries,
    kv_pages,
    page_table,
    seq_lengths,
    ffn_seat,
    resid,
    w_out,
    norm_gain,
    w_gate,
    w_up,
    w_down,
):
    seq_count = queries.shape[0]
    kv_local = kv_pages.shape[1]
    head_dim = kv_pages.shape[4]
    group_size = queries.shape[1] // (kv_local * head_dim)
    kv_blocks = kv_pages[page_table]
    key_span = kv_blocks.shape[1] * kv_blocks.shape[4]
    key_rows = (
        kv_blocks[:, :, :, 0]
        .transpose(0, 2, 1, 3, 4)
        .reshape(seq_count, kv_local, key_span, head_dim)
    )
    value_rows = (
        kv_blocks[:, :, :, 1]
        .transpose(0, 2, 1, 3, 4)
        .reshape(seq_count, kv_local, key_span, head_dim)
    )
    query_heads = queries.reshape(seq_count, kv_local, group_size, head_dim)
    scores = jnp.einsum(
        "skgd,sktd->skgt", query_heads, key_rows, preferred_element_type=jnp.float32
    ) * head_dim ** (-0.5)
    live_mask = jnp.arange(key_span)[None, :] < seq_lengths[:, None]
    scores = jnp.where(live_mask[:, None, None, :], scores, -1e30)
    top = jnp.max(scores, axis=-1, keepdims=True)
    expo = jnp.exp(scores - top)
    weights = (expo / jnp.sum(expo, axis=-1, keepdims=True)).astype(jnp.bfloat16)
    attended = jnp.einsum(
        "skgt,sktd->skgd", weights, value_rows, preferred_element_type=jnp.float32
    )
    attended = attended.astype(jnp.bfloat16).reshape(seq_count, -1)
    projected = jnp.dot(
        lax.all_gather(attended, "dev", axis=0, tiled=True),
        w_out,
        preferred_element_type=jnp.float32,
    )
    placed = jnp.zeros_like(projected).at[ffn_seat].set(projected)
    update = lax.psum_scatter(
        placed.astype(jnp.bfloat16), "col", scatter_dimension=0, tiled=True
    ).astype(jnp.float32)
    stream = resid.astype(jnp.float32) + update
    sq_total = lax.psum(jnp.sum(stream * stream, axis=1), "dev")
    full_width = stream.shape[1] * lax.axis_size("dev")
    normed = (
        stream * lax.rsqrt(sq_total / full_width + 1e-05)[:, None] * norm_gain[None, :]
    ).astype(jnp.bfloat16)
    block_rows = lax.all_gather(normed, "col", axis=0, tiled=True)
    gate_part = jnp.dot(block_rows, w_gate, preferred_element_type=jnp.float32)
    up_part = jnp.dot(block_rows, w_up, preferred_element_type=jnp.float32)
    gate_up = jnp.concatenate([gate_part, up_part], axis=1)
    half_width = w_gate.shape[1]
    shared_sums = lax.psum_scatter(
        gate_up.astype(jnp.bfloat16), "dev", scatter_dimension=0, tiled=True
    ).astype(jnp.float32)
    hidden_share = (jax.nn.silu(shared_sums[:, :half_width]) * shared_sums[:, half_width:]).astype(
        jnp.bfloat16
    )
    hidden = lax.all_gather(hidden_share, "dev", axis=0, tiled=True)
    ffn_out = lax.psum_scatter(
        jnp.dot(hidden, w_down, preferred_element_type=jnp.float32).astype(jnp.bfloat16),
        "col",
        scatter_dimension=0,
        tiled=True,
    ).astype(jnp.float32)
    return (stream + ffn_out).astype(jnp.bfloat16)


def solution(mesh):
    in_specs = (
        P(("rep", "dev"), "col"),
        P(("rep", "dev"), "col", None, None, None),
        P(("rep", "dev"), None),
        P(("rep", "dev")),
        P("rep"),
        P(("rep", "col"), "dev"),
        P("col", "dev"),
        P("dev"),
        P("dev", "col"),
        P("dev", "col"),
        P("col", "dev"),
    )
    out_specs = P(("rep", "col"), "dev")
    return jax.shard_map(
        on_device, mesh=mesh, in_specs=in_specs, out_specs=out_specs, check_vma=False
    )
```

profile of v0, /device:TPU:0, one launch (start us, length us, event | category | flops | bytes accessed | tf_op | source)
XLA Modules:
  0.0 218.6 jit_solution(14444316653443344116)
XLA Ops:
  7.4 11.5 %gather_fusion = bf16[96,2,2,128,128]{4,3,2,1,0:T(8,128)(2,1)} fusion(bf16[96,2,2,128,128]{4,3,2,1,0:T(8,128)(2,1)} %param.12, s32[1024]{0:T(1024)S(1)} %pad_clamp_fusion), kind=kCustom, calls=%fused_computation | custom fusion | bytes 25166208 | tf_op jit(solution)/shard_map/gather | solution.py:24
  18.9 5.3 %fusion.9 = (bf16[32,3,2,1,128,128]{5,4,3,2,1,0:T(8,128)(2,1)S(1)}, bf16[32,3,2,1,128,128]{5,4,3,2,1,0:T(8,128)(2,1)S(1)}) fusion(bf16[32,3,2,2,128,128]{5,4,3,2,1,0:T(8,128)(2,1)} %bitcast.34), kind=kLoop, calls=%fused_computation.29 | loop fusion | bytes 25165824 | tf_op jit(solution)/shard_map/slice | solution.py:27
  24.3 2.6 %copy.18 = bf16[32,3,2,1,128,128]{5,4,1,2,0,3:T(8,128)(2,1)S(1)} copy(bf16[32,3,2,1,128,128]{5,4,3,2,1,0:T(8,128)(2,1)S(1)} %get-tuple-element.5) | data formatting | bytes 12582912
  27.0 2.3 %fusion.4 = f32[32,2,8,384]{3,2,1,0:T(8,128)S(1)} fusion(bf16[32,2,384,128]{3,2,1,0:T(8,128)(2,1)S(1)} %bitcast.35, bf16[32,2,8,128]{3,2,1,0:T(8,128)(2,1)S(1)} %bitcast.37, pred[32,384]{1,0:T(8,128)(4,1)S(1)} %iota_compare_fusion), kind=kOutput, calls=%fused_computation.11 | convolution fusion | flops 50724864 | bytes 7221248 | tf_op jit(solution)/shard_map/skgd,sktd->skgt/dot_general | solution.py:37
  29.6 4.0 %copy.19 = bf16[32,3,2,1,128,128]{5,4,1,2,0,3:T(8,128)(2,1)} copy(bf16[32,3,2,1,128,128]{5,4,3,2,1,0:T(8,128)(2,1)S(1)} %get-tuple-element.6) | data formatting | bytes 12582912
  33.7 4.5 %convolution_convert_fusion.3 = bf16[32,2,8,128]{3,2,1,0:T(8,128)(2,1)S(1)} fusion(bf16[32,2,384,128]{3,2,1,0:T(8,128)(2,1)} %bitcast.36, f32[32,2,8]{2,1,0:T(2,128)S(1)} %fusion.10, f32[32,2,8,384]{3,2,1,0:T(8,128)} %copy-done), kind=kOutput, calls=%fused_computation.12 | convolution fusion | flops 50987904 | bytes 7211008 | tf_op jit(solution)/shard_map/skgt,sktd->skgd/dot_general | solution.py:45
  38.2 17.4 %all_gather.9 = bf16[128,2048]{1,0:T(8,128)(2,1)S(1)} all-gather(bf16[32,2048]{1,0:T(8,128)(2,1)S(1)} %bitcast.38), channel_id=1, replica_groups=mesh['rep'=2,'dev'=4,'col'=4] {'dev'}, dimensions={0}, use_global_device_ids=true | all-gather | bytes 655360 | tf_op jit(solution)/shard_map/all_gather | solution.py:50
  55.6 4.7 %fusion.11 = f32[128,2048]{1,0:T(8,128)S(1)} fusion(bf16[128,2048]{1,0:T(8,128)(2,1)S(1)} %all_gather.9, bf16[2048,2048]{1,0:T(8,128)(2,1)} %param.17), kind=kOutput, calls=%fused_computation.31 | convolution fusion | flops 1073741824 | bytes 9961472 | tf_op jit(solution)/shard_map/dot_general | solution.py:49
  60.3 1.5 scatter_custom_fusion
  61.8 0.9 convert_element_type.37
  62.8 23.5 %reduce-scatter.4.cloned.1.call-done = bf16[32,2048]{1,0:T(8,128)(2,1)} async-done(((bf16[128,2048]{1,0:T(8,128)(2,1)}), bf16[32,2048]{1,0:T(8,128)(2,1)}) %reduce-scatter.4.cloned.1.call-update) | async-done | bytes 131088 | tf_op jit(solution)/shard_map/reduce_scatter | solution.py:55
  86.3 1.1 multiply_reduce_fusion
  87.3 11.7 %psum.7 = f32[32]{0:T(128)S(1)} all-reduce(f32[32]{0:T(128)S(1)} %multiply_reduce_fusion), channel_id=1, replica_groups=mesh['rep'=2,'dev'=4,'col'=4] {'dev'}, use_global_device_ids=true, to_apply=%region_5.6 | all-reduce | flops 32 | bytes 256 | tf_op jit(solution)/shard_map/psum | solution.py:59
  99.0 1.0 multiply_convert_fusion
  100.0 6.7 %all_gather.10 = bf16[128,2048]{1,0:T(8,128)(2,1)S(1)} all-gather(bf16[32,2048]{1,0:T(8,128)(2,1)S(1)} %multiply_convert_fusion), channel_id=1, replica_groups=mesh['rep'=2,'dev'=4,'col'=4] {'col'}, dimensions={0}, use_global_device_ids=true | all-gather | bytes 655360 | tf_op jit(solution)/shard_map/all_gather | solution.py:64
  106.7 7.3 %convolution_convert_fusion = bf16[128,3584]{1,0:T(8,128)(2,1)S(1)} fusion(bf16[128,2048]{1,0:T(8,128)(2,1)S(1)} %all_gather.10, bf16[2048,3584]{1,0:T(8,128)(2,1)} %param.20), kind=kOutput, calls=%fused_computation.3 | convolution fusion | flops 1879506944 | bytes 16121856 | tf_op jit(solution)/shard_map/dot_general | solution.py:66
  114.0 7.3 %convolution_convert_fusion.1 = bf16[128,3584]{1,0:T(8,128)(2,1)S(1)} fusion(bf16[128,2048]{1,0:T(8,128)(2,1)S(1)} %all_gather.10, bf16[2048,3584]{1,0:T(8,128)(2,1)} %param.19), kind=kOutput, calls=%fused_computation.4 | convolution fusion | flops 1879506944 | bytes 16121856 | tf_op jit(solution)/shard_map/dot_general | solution.py:65
  121.3 1.4 pad_maximum_fusion
  122.8 37.5 %reduce-scatter.6.cloned.1.call-done = bf16[32,7168]{1,0:T(8,128)(2,1)} async-done(((bf16[128,7168]{1,0:T(8,128)(2,1)}), bf16[32,7168]{1,0:T(8,128)(2,1)}) %reduce-scatter.6.cloned.1.call-update) | async-done | bytes 458768 | tf_op jit(solution)/shard_map/reduce_scatter | solution.py:69
  160.3 1.1 convert_element_type.40
  161.5 19.1 %all_gather.11 = bf16[128,3584]{1,0:T(8,128)(2,1)S(1)} all-gather(bf16[32,3584]{1,0:T(8,128)(2,1)S(1)} %fusion.7), channel_id=1, replica_groups=mesh['rep'=2,'dev'=4,'col'=4] {'dev'}, dimensions={0}, use_global_device_ids=true | all-gather | bytes 1146880 | tf_op jit(solution)/shard_map/all_gather | solution.py:75
  180.6 8.3 %convolution_convert_fusion.2 = bf16[128,2048]{1,0:T(8,128)(2,1)} fusion(bf16[128,3584]{1,0:T(8,128)(2,1)S(1)} %all_gather.11, bf16[3584,2048]{1,0:T(8,128)(2,1)} %param.21), kind=kOutput, calls=%fused_computation.5 | convolution fusion | flops 1879310336 | bytes 16121856 | tf_op jit(solution)/shard_map/dot_general | solution.py:77
  189.0 21.5 %reduce-scatter.8.cloned.1.call-done = bf16[32,2048]{1,0:T(8,128)(2,1)} async-done(((bf16[128,2048]{1,0:T(8,128)(2,1)}), bf16[32,2048]{1,0:T(8,128)(2,1)}) %reduce-scatter.8.cloned.1.call-update) | async-done | bytes 131088 | tf_op jit(solution)/shard_map/reduce_scatter | solution.py:76
  210.4 1.6 add_convert_fusion
  (31 shorter events, 1.7 us)
Async XLA Ops:
  6.5 79.7 %reduce-scatter.4.cloned.1.call-start = ((), (), s32[]{:S(2)}) async-start(), calls=%async_computation.3 | async-start | bytes 655360 | tf_op jit(solution)/shard_map/reduce_scatter | solution.py:55
  24.2 2.7 %copy-start.3 = (bf16[32,2048]{1,0:T(8,128)(2,1)S(1)}, bf16[32,2048]{1,0:T(8,128)(2,1)}, u32[]{:S(2)}) copy-start(bf16[32,2048]{1,0:T(8,128)(2,1)} %param.11) | copy-start | bytes 393220
  24.2 2.7 %copy-start.5 = (s32[32]{0:T(128)S(1)}, s32[32]{0:T(128)}, u32[]{:S(2)}) copy-start(s32[32]{0:T(128)} %param.14) | copy-start | bytes 388
  29.3 4.4 %copy-start = (f32[32,2,8,384]{3,2,1,0:T(8,128)}, f32[32,2,8,384]{3,2,1,0:T(8,128)S(1)}, u32[]{:S(2)}) copy-start(f32[32,2,8,384]{3,2,1,0:T(8,128)S(1)} %fusion.4) | copy-start | bytes 2359300
  29.6 26.0 %copy-start.6 = (s32[128]{0:T(128)S(1)}, s32[128]{0:T(128)}, u32[]{:S(2)}) copy-start(s32[128]{0:T(128)} %param.15) | copy-start | bytes 1540
  55.6 30.7 %copy-start.1 = (bf16[32,2048]{1,0:T(8,128)(2,1)S(1)}, bf16[32,2048]{1,0:T(8,128)(2,1)}, u32[]{:S(2)}) copy-start(bf16[32,2048]{1,0:T(8,128)(2,1)} %param.16) | copy-start | bytes 393220
  55.6 43.4 %copy-start.4 = (f32[2048]{0:T(1024)S(1)}, f32[2048]{0:T(1024)}, u32[]{:S(2)}) copy-start(f32[2048]{0:T(1024)} %param.18) | copy-start | bytes 24580
  62.7 97.6 %reduce-scatter.6.cloned.1.call-start = ((), (), s32[]{:S(2)}) async-start(), calls=%async_computation.4 | async-start | bytes 2293760 | tf_op jit(solution)/shard_map/reduce_scatter | solution.py:69
  122.7 87.7 %reduce-scatter.8.cloned.1.call-start = ((), (), s32[]{:S(2)}) async-start(), calls=%async_computation.5 | async-start | bytes 655360 | tf_op jit(solution)/shard_map/reduce_scatter | solution.py:76
  180.6 29.9 %copy-start.2 = (bf16[32,2048]{1,0:T(8,128)(2,1)S(1)}, bf16[32,2048]{1,0:T(8,128)(2,1)}, u32[]{:S(2)}) copy-start(bf16[32,2048]{1,0:T(8,128)(2,1)} %reduce-scatter.4.cloned.1.call-done) | copy-start | bytes 393220
Sparse Core Ops, SparseCore 0:
  62.8 23.4 reduce-scatter.3
  122.8 37.3 reduce-scatter.5
  189.1 21.3 reduce-scatter.7
where the time goes:
time: 219 us
  waiting for transfers between devices  82.6 us (38%)
  blocking collectives  54.8 us (25%)
  matrix products  34.4 us (16%)
  local copies, waits for them, and re-layouts  25.2 us (12%)
  between operations  13.3 us (6%)
  other arithmetic  8.25 us (4%)
    reduce_scatter x1, waiting for transfers between devices, on_device(): lax.psum_scatter(gate_up.astype(jnp.bfloat16), 'dev', scatter_dimension=0...  37.5 us
    reduce_scatter x1, waiting for transfers between devices, on_device(): lax.psum_scatter(placed.astype(jnp.bfloat16), 'col', scatter_dimension=0,...  23.5 us
    reduce_scatter x1, waiting for transfers between devices, on_device(): lax.psum_scatter(jnp.dot(hidden, w_down, preferred_element_type=jnp.float...  21.5 us
    all_gather x1, blocking collectives, on_device(): hidden = lax.all_gather(hidden_share, 'dev', axis=0, tiled=True)  19.1 us
    all_gather x1, blocking collectives, on_device(): lax.all_gather(attended, 'dev', axis=0, tiled=True)  17.4 us
    psum x1, blocking collectives, on_device(): sq_total = lax.psum(jnp.sum(stream * stream, axis=1), 'dev')  11.7 us
    gather x1, local copies, waits for them, and re-layouts, on_device(): kv_blocks = kv_pages[page_table]  11.5 us
    dot_general x1, matrix products, on_device(): jnp.dot(hidden, w_down, preferred_element_type=jnp.float32)  8.35 us
  transfers between devices with their start and end apart: 3, of which 3 were waited for; matrix products, arithmetic and copies ran while one was open for 0% of the time, Pallas kernels for 0%

commit v1 on v0

--- a/solution.py
+++ b/solution.py
@@ -2,6 +2,10 @@
 import jax.numpy as jnp
 from jax import lax
 from jax.sharding import PartitionSpec as P
+
+
+def push_quotas(v0):
+    return jnp.sum(jax.lax.all_gather(v0, axis_name="dev"), axis=0)
 
 
 def on_device(
@@ -56,7 +60,7 @@
         placed.astype(jnp.bfloat16), "col", scatter_dimension=0, tiled=True
     ).astype(jnp.float32)
     stream = resid.astype(jnp.float32) + update
-    sq_total = lax.psum(jnp.sum(stream * stream, axis=1), "dev")
+    sq_total = push_quotas(jnp.sum(stream * stream, axis=1))
     full_width = stream.shape[1] * lax.axis_size("dev")
     normed = (
         stream * lax.rsqrt(sq_total / full_width + 1e-05)[:, None] * norm_gain[None, :]

time: 219 us -> 219 us (level)
    psum x1 -> x0, blocking collectives: 11.7 us -> none  [on_device(): sq_total = lax.psum(jnp.sum(stream * stream, axis=1), 'dev')]
    unnamed x0 -> x1, blocking collectives: none -> 11.7 us
    unnamed x18 -> x23, local copies, waits for them, and re-layouts: 6.78 us -> 7.61 us
where the time goes in v1:
time: 219 us
  waiting for transfers between devices  81.3 us (37%)
  blocking collectives  54.8 us (25%)
  matrix products  34.4 us (16%)
  local copies, waits for them, and re-layouts  26.2 us (12%)
  between operations  13.9 us (6%)
  other arithmetic  8.27 us (4%)
    reduce_scatter x1, waiting for transfers between devices, on_device(): lax.psum_scatter(gate_up.astype(jnp.bfloat16), 'dev', scatter_dimension=0...  37.5 us
    reduce_scatter x1, waiting for transfers between devices, on_device(): lax.psum_scatter(placed.astype(jnp.bfloat16), 'col', scatter_dimension=0,...  22.2 us
    reduce_scatter x1, waiting for transfers between devices, on_device(): lax.psum_scatter(jnp.dot(hidden, w_down, preferred_element_type=jnp.float...  21.5 us
    all_gather x1, blocking collectives, on_device(): hidden = lax.all_gather(hidden_share, 'dev', axis=0, tiled=True)  19.1 us
    all_gather x1, blocking collectives, on_device(): lax.all_gather(attended, 'dev', axis=0, tiled=True)  17.4 us
    unnamed x1, blocking collectives  11.7 us
    gather x1, local copies, waits for them, and re-layouts, on_device(): kv_blocks = kv_pages[page_table]  11.5 us
    dot_general x1, matrix products, on_device(): jnp.dot(hidden, w_down, preferred_element_type=jnp.float32)  8.35 us
  transfers between devices with their start and end apart: 3, of which 3 were waited for; matrix products, arithmetic and copies ran while one was open for 0% of the time, Pallas kernels for 0%

profile of v1, /device:TPU:0, one launch (start us, length us, event | category | flops | bytes accessed | tf_op | source)
XLA Modules:
  0.0 218.9 jit_solution(10186314834505629324)
XLA Ops:
  7.4 11.5 %gather_fusion = bf16[96,2,2,128,128]{4,3,2,1,0:T(8,128)(2,1)} fusion(bf16[96,2,2,128,128]{4,3,2,1,0:T(8,128)(2,1)} %param.12, s32[1024]{0:T(1024)S(1)} %pad_clamp_fusion), kind=kCustom, calls=%fused_computation | custom fusion | bytes 25166208 | tf_op jit(solution)/shard_map/gather | solution.py:28
  18.9 5.3 %fusion.9 = (bf16[32,3,2,1,128,128]{5,4,3,2,1,0:T(8,128)(2,1)S(1)}, bf16[32,3,2,1,128,128]{5,4,3,2,1,0:T(8,128)(2,1)S(1)}) fusion(bf16[32,3,2,2,128,128]{5,4,3,2,1,0:T(8,128)(2,1)} %bitcast.35), kind=kLoop, calls=%fused_computation.29 | loop fusion | bytes 25165824 | tf_op jit(solution)/shard_map/slice | solution.py:31
  24.3 2.6 %copy.18 = bf16[32,3,2,1,128,128]{5,4,1,2,0,3:T(8,128)(2,1)S(1)} copy(bf16[32,3,2,1,128,128]{5,4,3,2,1,0:T(8,128)(2,1)S(1)} %get-tuple-element.5) | data formatting | bytes 12582912
  27.0 2.3 %fusion.4 = f32[32,2,8,384]{3,2,1,0:T(8,128)S(1)} fusion(bf16[32,2,384,128]{3,2,1,0:T(8,128)(2,1)S(1)} %bitcast.36, bf16[32,2,8,128]{3,2,1,0:T(8,128)(2,1)S(1)} %bitcast.38, pred[32,384]{1,0:T(8,128)(4,1)S(1)} %iota_compare_fusion), kind=kOutput, calls=%fused_computation.11 | convolution fusion | flops 50724864 | bytes 7221248 | tf_op jit(solution)/shard_map/skgd,sktd->skgt/dot_general | solution.py:41
  29.6 4.0 %copy.19 = bf16[32,3,2,1,128,128]{5,4,1,2,0,3:T(8,128)(2,1)} copy(bf16[32,3,2,1,128,128]{5,4,3,2,1,0:T(8,128)(2,1)S(1)} %get-tuple-element.6) | data formatting | bytes 12582912
  33.7 4.5 %convolution_convert_fusion.3 = bf16[32,2,8,128]{3,2,1,0:T(8,128)(2,1)S(1)} fusion(bf16[32,2,384,128]{3,2,1,0:T(8,128)(2,1)} %bitcast.37, f32[32,2,8]{2,1,0:T(2,128)S(1)} %fusion.10, f32[32,2,8,384]{3,2,1,0:T(8,128)} %copy-done), kind=kOutput, calls=%fused_computation.12 | convolution fusion | flops 50987904 | bytes 7211008 | tf_op jit(solution)/shard_map/skgt,sktd->skgd/dot_general | solution.py:49
  38.2 17.4 %all_gather.15 = bf16[128,2048]{1,0:T(8,128)(2,1)S(1)} all-gather(bf16[32,2048]{1,0:T(8,128)(2,1)S(1)} %bitcast.39), channel_id=1, replica_groups=mesh['rep'=2,'dev'=4,'col'=4] {'dev'}, dimensions={0}, use_global_device_ids=true | all-gather | bytes 655360 | tf_op jit(solution)/shard_map/all_gather | solution.py:54
  55.6 4.7 %fusion.11 = f32[128,2048]{1,0:T(8,128)S(1)} fusion(bf16[128,2048]{1,0:T(8,128)(2,1)S(1)} %all_gather.15, bf16[2048,2048]{1,0:T(8,128)(2,1)} %param.17), kind=kOutput, calls=%fused_computation.31 | convolution fusion | flops 1073741824 | bytes 9961472 | tf_op jit(solution)/shard_map/dot_general | solution.py:53
  60.4 1.5 scatter_custom_fusion
  61.8 0.9 convert_element_type.37
  64.0 22.2 %reduce-scatter.4.cloned.1.call-done = bf16[32,2048]{1,0:T(8,128)(2,1)} async-done(((bf16[128,2048]{1,0:T(8,128)(2,1)}), bf16[32,2048]{1,0:T(8,128)(2,1)}) %reduce-scatter.4.cloned.1.call-update) | async-done | bytes 131088 | tf_op jit(solution)/shard_map/reduce_scatter | solution.py:59
  86.3 1.1 multiply_reduce_fusion
  87.6 11.7 %all-reduce = f32[128]{0:T(128)S(1)} all-reduce(f32[128]{0:T(128)S(1)} %dynamic-update-slice), channel_id=2, replica_groups=mesh['rep'=2,'dev'=4,'col'=4] {'dev'}, use_global_device_ids=true, to_apply=%add | all-reduce | flops 128 | bytes 1024
  99.4 1.0 multiply_convert_fusion
  100.4 6.7 %all_gather.18 = bf16[128,2048]{1,0:T(8,128)(2,1)S(1)} all-gather(bf16[32,2048]{1,0:T(8,128)(2,1)S(1)} %multiply_convert_fusion), channel_id=1, replica_groups=mesh['rep'=2,'dev'=4,'col'=4] {'col'}, dimensions={0}, use_global_device_ids=true | all-gather | bytes 655360 | tf_op jit(solution)/shard_map/all_gather | solution.py:68
  107.1 7.3 %convolution_convert_fusion = bf16[128,3584]{1,0:T(8,128)(2,1)S(1)} fusion(bf16[128,2048]{1,0:T(8,128)(2,1)S(1)} %all_gather.18, bf16[2048,3584]{1,0:T(8,128)(2,1)} %param.20), kind=kOutput, calls=%fused_computation.3 | convolution fusion | flops 1879506944 | bytes 16121856 | tf_op jit(solution)/shard_map/dot_general | solution.py:70
  114.3 7.3 %convolution_convert_fusion.1 = bf16[128,3584]{1,0:T(8,128)(2,1)S(1)} fusion(bf16[128,2048]{1,0:T(8,128)(2,1)S(1)} %all_gather.18, bf16[2048,3584]{1,0:T(8,128)(2,1)} %param.19), kind=kOutput, calls=%fused_computation.4 | convolution fusion | flops 1879506944 | bytes 16121856 | tf_op jit(solution)/shard_map/dot_general | solution.py:69
  121.6 1.4 pad_maximum_fusion
  123.1 37.5 %reduce-scatter.6.cloned.1.call-done = bf16[32,7168]{1,0:T(8,128)(2,1)} async-done(((bf16[128,7168]{1,0:T(8,128)(2,1)}), bf16[32,7168]{1,0:T(8,128)(2,1)}) %reduce-scatter.6.cloned.1.call-update) | async-done | bytes 458768 | tf_op jit(solution)/shard_map/reduce_scatter | solution.py:73
  160.6 1.1 convert_element_type.40
  161.8 19.1 %all_gather.19 = bf16[128,3584]{1,0:T(8,128)(2,1)S(1)} all-gather(bf16[32,3584]{1,0:T(8,128)(2,1)S(1)} %fusion.7), channel_id=1, replica_groups=mesh['rep'=2,'dev'=4,'col'=4] {'dev'}, dimensions={0}, use_global_device_ids=true | all-gather | bytes 1146880 | tf_op jit(solution)/shard_map/all_gather | solution.py:79
  181.0 8.3 %convolution_convert_fusion.2 = bf16[128,2048]{1,0:T(8,128)(2,1)} fusion(bf16[128,3584]{1,0:T(8,128)(2,1)S(1)} %all_gather.19, bf16[3584,2048]{1,0:T(8,128)(2,1)} %param.21), kind=kOutput, calls=%fused_computation.5 | convolution fusion | flops 1879310336 | bytes 16121856 | tf_op jit(solution)/shard_map/dot_general | solution.py:81
  189.3 21.5 %reduce-scatter.8.cloned.1.call-done = bf16[32,2048]{1,0:T(8,128)(2,1)} async-done(((bf16[128,2048]{1,0:T(8,128)(2,1)}), bf16[32,2048]{1,0:T(8,128)(2,1)}) %reduce-scatter.8.cloned.1.call-update) | async-done | bytes 131088 | tf_op jit(solution)/shard_map/reduce_scatter | solution.py:80
  210.8 1.6 add_convert_fusion
  (38 shorter events, 2.6 us)
Async XLA Ops:
  6.5 79.7 %reduce-scatter.4.cloned.1.call-start = ((), (), s32[]{:S(2)}) async-start(), calls=%async_computation.3 | async-start | bytes 655360 | tf_op jit(solution)/shard_map/reduce_scatter | solution.py:59
  24.2 2.7 %copy-start.3 = (bf16[32,2048]{1,0:T(8,128)(2,1)S(1)}, bf16[32,2048]{1,0:T(8,128)(2,1)}, u32[]{:S(2)}) copy-start(bf16[32,2048]{1,0:T(8,128)(2,1)} %param.11) | copy-start | bytes 393220
  24.2 2.7 %copy-start.5 = (s32[32]{0:T(128)S(1)}, s32[32]{0:T(128)}, u32[]{:S(2)}) copy-start(s32[32]{0:T(128)} %param.14) | copy-start | bytes 388
  29.3 4.4 %copy-start = (f32[32,2,8,384]{3,2,1,0:T(8,128)}, f32[32,2,8,384]{3,2,1,0:T(8,128)S(1)}, u32[]{:S(2)}) copy-start(f32[32,2,8,384]{3,2,1,0:T(8,128)S(1)} %fusion.4) | copy-start | bytes 2359300
  29.6 26.0 %copy-start.6 = (s32[128]{0:T(128)S(1)}, s32[128]{0:T(128)}, u32[]{:S(2)}) copy-start(s32[128]{0:T(128)} %param.15) | copy-start | bytes 1540
  55.6 7.2 %copy-start.7 = (u32[32]{0:T(128)S(1)}, u32[32]{0:T(128)}, u32[]{:S(2)}) copy-start(u32[32]{0:T(128)} %constant.27) | copy-start | bytes 388
  55.6 30.6 %copy-start.1 = (bf16[32,2048]{1,0:T(8,128)(2,1)S(1)}, bf16[32,2048]{1,0:T(8,128)(2,1)}, u32[]{:S(2)}) copy-start(bf16[32,2048]{1,0:T(8,128)(2,1)} %param.16) | copy-start | bytes 393220
  55.6 43.7 %copy-start.4 = (f32[2048]{0:T(1024)S(1)}, f32[2048]{0:T(1024)}, u32[]{:S(2)}) copy-start(f32[2048]{0:T(1024)} %param.18) | copy-start | bytes 24580
  62.7 97.9 %reduce-scatter.6.cloned.1.call-start = ((), (), s32[]{:S(2)}) async-start(), calls=%async_computation.4 | async-start | bytes 2293760 | tf_op jit(solution)/shard_map/reduce_scatter | solution.py:73
  123.1 87.7 %reduce-scatter.8.cloned.1.call-start = ((), (), s32[]{:S(2)}) async-start(), calls=%async_computation.5 | async-start | bytes 655360 | tf_op jit(solution)/shard_map/reduce_scatter | solution.py:80
  180.9 29.9 %copy-start.2 = (bf16[32,2048]{1,0:T(8,128)(2,1)S(1)}, bf16[32,2048]{1,0:T(8,128)(2,1)}, u32[]{:S(2)}) copy-start(bf16[32,2048]{1,0:T(8,128)(2,1)} %reduce-scatter.4.cloned.1.call-done) | copy-start | bytes 393220
Sparse Core Ops, SparseCore 0:
  62.8 23.3 reduce-scatter.3
  123.2 37.3 reduce-scatter.5
  189.4 21.3 reduce-scatter.7
